TPU v7x, 32 devices: a whole 2x2x4 slice. The times are simulated.
32 devices in a mesh: ep: 8 (over y, x, core), dp: 4 (over z).
Axes of the slice: x: 2, y: 2, z: 4, core: 2. Of those that a mesh axis runs over, the one named last changes fastest.
Arguments:
- tokens: bfloat16 [64, 7168], P('dp', 'ep'), may hold values from -6 to 6
- norm_gain: float32 [2, 7168], replicated, may hold values from 0.1 to 1.9
- gate_weight: bfloat16 [2, 12, 2048, 7168], P(None, 'dp', 'ep'), may hold values from -0.0625 to 0.0625
- up_weight: bfloat16 [2, 12, 2048, 7168], P(None, 'dp', 'ep'), may hold values from -0.0625 to 0.0625
- down_weight: bfloat16 [2, 12, 7168, 2048], P(None, 'dp', 'ep'), may hold values from -0.125 to 0.125
- replica_plan: int32 [2, 4, 2], replicated, may hold values from 0 to 2
- route_expert: int32 [2, 64, 8], replicated, may hold values from 0 to 11, as said below
- replica_pick: int32 [2, 64, 8], replicated, may hold values from 0 to 2
- combine_num: int32 [2, 64, 8], P(None, 'dp'), may hold values from 1 to 8
Outputs:
- stream_out: bfloat16 [64, 7168], P('dp', 'ep')
- last_update: bfloat16 [64, 7168], P('dp', 'ep')
Inputs may be any that keep to these rules, and one draw needn't show every extreme that they name: `route_expert`: each row of one layer names 8 different experts.
All inputs are finite; a program needn't handle non-finite values.
Results may differ from a plain program's by a relative error of at most 0.011.
Values may be sent and summed in bfloat16 or wider, within the bound.
A program may use at most 256 MiB of HBM per device.

v0:
```python
import jax
import jax.numpy as jnp
from jax import lax
from jax.sharding import PartitionSpec as P

epsilon = 1e-06


def serve_table(plan_layer, host_count, exp_host, rep_host):
    replicas = exp_host + rep_host
    flat_ids = jnp.arange(host_count * replicas, dtype=jnp.int32)
    host_of = flat_ids // replicas
    local_id = flat_ids % replicas
    copy_id = jnp.clip(local_id - exp_host, 0, rep_host - 1)
    owner = (host_of - 1 - copy_id) % host_count
    copied = owner * exp_host + plan_layer[host_of, copy_id]
    return jnp.where(local_id < exp_host, host_of * exp_host + local_id, copied)


def targets(experts_g, picks_g, table):
    flat_e = experts_g.reshape(-1)
    flat_p = picks_g.reshape(-1)
    matches = (table[None, :] == flat_e[:, None]).astype(jnp.int32)
    counts = jnp.sum(matches, axis=1)
    rank_in = jnp.cumsum(matches, axis=1) - 1
    wanted = flat_p % counts
    chosen = matches * (rank_in == wanted[:, None]).astype(jnp.int32)
    target = jnp.sum(chosen * jnp.arange(table.shape[0], dtype=jnp.int32)[None, :], axis=1)
    before = jnp.cumsum(chosen, axis=0) - chosen
    position = jnp.sum(before * chosen, axis=1)
    return (target, position)


def per_device(
    tokens,
    norm_gain,
    gate_weight,
    up_weight,
    down_weight,
    replica_plan,
    route_expert,
    replica_pick,
    combine_num,
):
    host_count = lax.axis_size("dp")
    host_index = lax.axis_index("dp")
    column_index = lax.axis_index("ep")
    layer_count = norm_gain.shape[0]
    width = norm_gain.shape[1]
    exp_host = gate_weight.shape[1]
    rep_host = replica_plan.shape[2]
    replicas = exp_host + rep_host
    group_rows = tokens.shape[0]
    top_count = route_expert.shape[2]
    capacity = group_rows // 2
    slice_width = tokens.shape[1]
    unit_count = gate_weight.shape[2]
    slot_count = host_count * capacity
    buffer_rows = host_count * replicas * capacity
    row_ids = jnp.arange(buffer_rows, dtype=jnp.int32)
    act_shape = (replicas, unit_count, host_count, capacity)
    stream = tokens
    update = jnp.zeros((group_rows, slice_width), jnp.float32)
    for layer_id in range(layer_count):
        extra = [
            replica_plan[layer_id, (host_index + 1 + copy_id) % host_count, copy_id]
            for copy_id in range(rep_host)
        ]
        chosen_ids = jnp.concatenate([jnp.arange(exp_host, dtype=jnp.int32), jnp.stack(extra)])
        gate_all = gate_weight[layer_id][chosen_ids]
        up_all = up_weight[layer_id][chosen_ids]
        down_all = down_weight[layer_id][chosen_ids]
        table = serve_table(replica_plan[layer_id], host_count, exp_host, rep_host)
        grouped_e = route_expert[layer_id].reshape(host_count, group_rows, top_count)
        grouped_p = replica_pick[layer_id].reshape(host_count, group_rows, top_count)
        every_target, every_position = jax.vmap(lambda e_blk, p_blk: targets(e_blk, p_blk, table))(
            grouped_e, grouped_p
        )
        owner_of = every_target // replicas
        slot_of = every_target % replicas
        destination_copy_id = jnp.clip(slot_of - exp_host, 0, rep_host - 1)
        moved = (owner_of - 1 - destination_copy_id) % host_count
        every_dest = jnp.where(slot_of < exp_host, owner_of, moved)
        every_slot = every_target % replicas
        dest = lax.dynamic_index_in_dim(every_dest, host_index, 0, keepdims=False)
        slot_of = lax.dynamic_index_in_dim(every_slot, host_index, 0, keepdims=False)
        position = lax.dynamic_index_in_dim(every_position, host_index, 0, keepdims=False)
        kept = position < capacity
        stream_f = stream.astype(jnp.float32)
        squares = lax.psum(jnp.sum(stream_f * stream_f, axis=1), "ep")
        inverse_rms = lax.rsqrt(squares / width + epsilon)
        gain_part = lax.dynamic_slice_in_dim(
            norm_gain[layer_id], column_index * slice_width, slice_width, 0
        )
        normed = (stream_f * inverse_rms[:, None] * gain_part[None, :]).astype(jnp.bfloat16)
        buffer_index = jnp.where(
            kept, dest * (replicas * capacity) + slot_of * capacity + position, -1
        ).reshape(group_rows, top_count)
        select = jnp.any(row_ids[:, None, None] == buffer_index[None, :, :], axis=2).astype(
            jnp.bfloat16
        )
        packed = jnp.dot(select, normed, preferred_element_type=jnp.float32).astype(jnp.bfloat16)
        packed = packed.reshape(host_count, replicas, capacity, slice_width)
        received = lax.all_to_all(packed, "dp", split_axis=0, concat_axis=0, tiled=True)
        portion = lax.all_gather(received, "ep", axis=3, tiled=True)
        gate_new = jnp.einsum(
            "srcd,rfd->rfsc", portion, gate_all, preferred_element_type=jnp.float32
        ).reshape(-1)
        up_new = jnp.einsum(
            "srcd,rfd->rfsc", portion, up_all, preferred_element_type=jnp.float32
        ).reshape(-1)
        gate_act = gate_new.reshape(act_shape)
        up_act = up_new.reshape(act_shape)
        hidden = (
            (jax.nn.silu(gate_act) * up_act)
            .astype(jnp.bfloat16)
            .reshape(replicas, unit_count, slot_count)
        )
        result = jnp.einsum(
            "rfs,rdf->rsd",
            lax.all_gather(hidden, "ep", axis=1, tiled=True),
            down_all,
            preferred_element_type=jnp.float32,
        ).reshape(-1)
        result = result.astype(jnp.bfloat16).reshape(replicas, host_count, capacity, slice_width)
        returned = lax.all_to_all(result, "dp", split_axis=1, concat_axis=1, tiled=True)
        flat_rows = returned.reshape(replicas * host_count * capacity, slice_width)
        row_pick = slot_of * slot_count + dest * capacity + jnp.minimum(position, capacity - 1)
        picked = flat_rows[row_pick].astype(jnp.float32).reshape(group_rows, top_count, slice_width)
        numerator = combine_num[layer_id].astype(jnp.float32)
        weights_k = numerator / jnp.sum(numerator, axis=1, keepdims=True)
        combine = weights_k * kept.reshape(group_rows, top_count).astype(jnp.float32)
        update = jnp.sum(combine[:, :, None] * picked, axis=1)
        stream = (stream_f + update).astype(jnp.bfloat16)
    return (stream, update.astype(jnp.bfloat16))


def solution(mesh):
    return jax.shard_map(
        per_device,
        mesh=mesh,
        in_specs=(
            P("dp", "ep"),
            P(),
            P(None, "dp", "ep", None),
            P(None, "dp", "ep", None),
            P(None, "dp", "ep", None),
            P(),
            P(),
            P(),
            P(None, "dp", None),
        ),
        out_specs=(P("dp", "ep"), P("dp", "ep")),
        check_vma=False,
    )
```

profile of v0, /device:TPU:0, one launch (start us, length us, event | category | flops | bytes accessed | tf_op | source)
XLA Modules:
  0.0 353.5 jit_solution(13358353863704783051)
XLA Ops:
  16.1 15.1 %psum.14 = f32[16]{0:T(128)S(1)} all-reduce(f32[16]{0:T(128)S(1)} %fusion.34), channel_id=1, replica_groups=mesh['ep'=8,'dp'=4] {'ep'}, use_global_device_ids=true, to_apply=%region_8.9 | all-reduce | flops 16 | bytes 128 | tf_op jit(solution)/shard_map/psum | solution.py:90
  37.9 8.7 %slice_bitcast_fusion.2 = (bf16[3,256,7168]{2,1,0:T(8,128)(2,1)S(1)}, bf16[3,256,7168]{2,1,0:T(8,128)(2,1)S(1)}) fusion(bf16[2,3,256,7168]{3,2,1,0:T(8,128)(2,1)} %param.11), kind=kLoop, calls=%fused_computation.34 | loop fusion | bytes 44040192 | tf_op jit(solution)/shard_map/squeeze | solution.py:70
  46.7 15.5 %slice_bitcast_fusion.1 = (bf16[3,256,7168]{2,1,0:T(8,128)(2,1)}, bf16[3,256,7168]{2,1,0:T(8,128)(2,1)}) fusion(bf16[2,3,256,7168]{3,2,1,0:T(8,128)(2,1)} %param.12), kind=kLoop, calls=%fused_computation.33 | loop fusion | bytes 44040192 | tf_op jit(solution)/shard_map/squeeze | solution.py:71
  89.5 16.0 %fusion.83 = (bf16[3,256,3584]{2,1,0:T(8,128)(2,1)}, bf16[3,256,3584]{2,1,0:T(8,128)(2,1)}, bf16[3,256,3584]{2,1,0:T(8,128)(2,1)}, bf16[3,256,3584]{2,1,0:T(8,128)(2,1)}) fusion(bf16[3,256,7168]{2,1,0:T(8,128)(2,1)} %get-tuple-element.14, bf16[3,256,7168]{2,1,0:T(8,128)(2,1)} %get-tuple-element.15), kind=kLoop, calls=%fused_computation.190 | loop fusion | bytes 44040192 | tf_op jit(solution)/shard_map/gather | solution.py:71
  121.1 9.0 %slice_bitcast_fusion = (bf16[3,896,2048]{2,1,0:T(8,128)(2,1)S(1)}, bf16[3,896,2048]{2,1,0:T(8,128)(2,1)S(1)}) fusion(bf16[2,3,896,2048]{3,2,1,0:T(8,128)(2,1)} %param.13), kind=kLoop, calls=%fused_computation.32 | loop fusion | bytes 44040192 | tf_op jit(solution)/shard_map/squeeze | solution.py:72
  138.0 7.8 %gather_fusion.8 = bf16[5,896,1024]{2,1,0:T(8,128)(2,1)} fusion(bf16[3,896,1024]{2,1,0:T(8,128)(2,1)} %get-tuple-element.59, s32[1024]{0:T(1024)S(1)} %pad_clamp_fusion.3), kind=kCustom, calls=%fused_computation.8 | custom fusion | bytes 18350100 | tf_op jit(solution)/shard_map/gather | solution.py:72
  153.9 10.3 %fusion.11 = f32[5,256,4,8]{1,3,2,0:T(8,128)S(1)} fusion(bf16[4,5,8,7168]{3,2,0,1:T(8,128)(2,1)} %all-gather.3.cloned.1.call-done, bf16[5,256,3584]{2,1,0:T(8,128)(2,1)} %gather_fusion.5, bf16[5,256,3584]{2,1,0:T(8,128)(2,1)} %gather_fusion.4), kind=kOutput, calls=%fused_computation.31 | convolution fusion | flops 623902720 | bytes 20807680 | tf_op jit(solution)/shard_map/srcd,rfd->rfsc/dot_general | solution.py:106
  164.2 10.5 %fusion.29 = bf16[5,256,32]{1,2,0:T(8,128)(2,1)S(1)} fusion(bf16[4,5,8,7168]{3,2,0,1:T(8,128)(2,1)} %all-gather.3.cloned.1.call-done, bf16[5,256,3584]{2,1,0:T(8,128)(2,1)} %gather_fusion.7, bf16[5,256,3584]{2,1,0:T(8,128)(2,1)} %gather_fusion.6, f32[5,256,4,8]{1,3,2,0:T(8,128)S(1)} %fusion.11), kind=kOutput, calls=%fused_computation.49 | convolution fusion | flops 624148480 | bytes 20889600 | tf_op jit(solution)/shard_map/srcd,rfd->rfsc/dot_general | solution.py:109
  174.8 10.5 %all_gather.13 = bf16[5,2048,32]{1,2,0:T(8,128)(2,1)S(1)} all-gather(bf16[5,256,32]{1,2,0:T(8,128)(2,1)S(1)} %fusion.29), channel_id=1, replica_groups=mesh['ep'=8,'dp'=4] {'ep'}, dimensions={1}, use_global_device_ids=true | all-gather | bytes 737280 | tf_op jit(solution)/shard_map/all_gather | solution.py:121
  185.3 10.5 %fusion.18 = bf16[5,4,8,896]{3,2,1,0:T(8,128)(2,1)S(1)} fusion(bf16[5,2048,32]{1,2,0:T(8,128)(2,1)S(1)} %all_gather.13, bf16[5,896,1024]{2,1,0:T(8,128)(2,1)} %gather_fusion.9, bf16[5,896,1024]{2,1,0:T(8,128)(2,1)} %gather_fusion.8), kind=kOutput, calls=%fused_computation.42 | convolution fusion | flops 624046080 | bytes 19292160 | tf_op jit(solution)/shard_map/rfs,rdf->rsd/dot_general | solution.py:119
  203.3 9.7 %all-to-all-done.1 = bf16[5,4,8,896]{3,2,0,1:T(8,128)(2,1)S(1)} async-done(((bf16[5,4,8,896]{3,2,0,1:T(8,128)(2,1)}), bf16[5,4,8,896]{3,2,0,1:T(8,128)(2,1)S(1)}, u32[]{:S(2)}, u32[]{:S(2)}) %all-to-all-start.1) | async-done | bytes 286752 | tf_op jit(solution)/shard_map/all_to_all | solution.py:126
  214.2 11.8 %psum.15 = f32[16]{0:T(128)S(1)} all-reduce(f32[16]{0:T(128)S(1)} %get-tuple-element.8), channel_id=1, replica_groups=mesh['ep'=8,'dp'=4] {'ep'}, use_global_device_ids=true, to_apply=%region_18.19 | all-reduce | flops 16 | bytes 128 | tf_op jit(solution)/shard_map/psum | solution.py:90
  226.3 12.1 %all_to_all.20 = bf16[4,5,8,896]{3,2,1,0:T(8,128)(2,1)S(1)} all-to-all(bf16[4,5,8,896]{3,2,1,0:T(8,128)(2,1)S(1)} %bitcast.98), channel_id=1, replica_groups=mesh['ep'=8,'dp'=4] {'dp'}, dimensions={0} | all-to-all | bytes 573440 | tf_op jit(solution)/shard_map/all_to_all | solution.py:104
  239.2 8.2 %gather_fusion.10 = bf16[5,256,3584]{2,1,0:T(8,128)(2,1)} fusion(bf16[3,256,3584]{2,1,0:T(8,128)(2,1)} %get-tuple-element.18, s32[1024]{0:T(1024)S(1)} %pad_clamp_fusion.1), kind=kCustom, calls=%fused_computation.10 | custom fusion | bytes 18350100 | tf_op jit(solution)/shard_map/gather | solution.py:70
  247.4 8.1 %gather_fusion.11 = bf16[5,256,3584]{2,1,0:T(8,128)(2,1)} fusion(bf16[3,256,3584]{2,1,0:T(8,128)(2,1)} %get-tuple-element.19, s32[1024]{0:T(1024)S(1)} %pad_clamp_fusion.1), kind=kCustom, calls=%fused_computation.11 | custom fusion | bytes 18350100 | tf_op jit(solution)/shard_map/gather | solution.py:70
  255.4 8.5 %gather_fusion.12 = bf16[5,256,3584]{2,1,0:T(8,128)(2,1)} fusion(bf16[3,256,3584]{2,1,0:T(8,128)(2,1)} %get-tuple-element.20, s32[1024]{0:T(1024)S(1)} %pad_clamp_fusion.1), kind=kCustom, calls=%fused_computation.12 | custom fusion | bytes 18350100 | tf_op jit(solution)/shard_map/gather | solution.py:71
  263.9 8.0 %gather_fusion.13 = bf16[5,256,3584]{2,1,0:T(8,128)(2,1)} fusion(bf16[3,256,3584]{2,1,0:T(8,128)(2,1)} %get-tuple-element.21, s32[1024]{0:T(1024)S(1)} %pad_clamp_fusion.1), kind=kCustom, calls=%fused_computation.13 | custom fusion | bytes 18350100 | tf_op jit(solution)/shard_map/gather | solution.py:71
  271.9 8.1 %gather_fusion.14 = bf16[5,896,1024]{2,1,0:T(8,128)(2,1)} fusion(bf16[3,896,1024]{2,1,0:T(8,128)(2,1)} %get-tuple-element.16, s32[1024]{0:T(1024)S(1)} %pad_clamp_fusion.1), kind=kCustom, calls=%fused_computation.14 | custom fusion | bytes 18350100 | tf_op jit(solution)/shard_map/gather | solution.py:72
  280.0 8.0 %gather_fusion.15 = bf16[5,896,1024]{2,1,0:T(8,128)(2,1)} fusion(bf16[3,896,1024]{2,1,0:T(8,128)(2,1)} %get-tuple-element.17, s32[1024]{0:T(1024)S(1)} %pad_clamp_fusion.1), kind=kCustom, calls=%fused_computation.15 | custom fusion | bytes 18350100 | tf_op jit(solution)/shard_map/gather | solution.py:72
  288.1 10.3 %fusion.9 = f32[5,256,4,8]{1,3,2,0:T(8,128)S(1)} fusion(bf16[4,5,8,7168]{3,2,0,1:T(8,128)(2,1)} %all-gather.5.cloned.1.call-done, bf16[5,256,3584]{2,1,0:T(8,128)(2,1)} %gather_fusion.11, bf16[5,256,3584]{2,1,0:T(8,128)(2,1)} %gather_fusion.10), kind=kOutput, calls=%fused_computation.29 | convolution fusion | flops 623902720 | bytes 20807680 | tf_op jit(solution)/shard_map/srcd,rfd->rfsc/dot_general | solution.py:106
  298.3 10.3 %fusion.28 = bf16[5,256,32]{1,2,0:T(8,128)(2,1)S(1)} fusion(bf16[4,5,8,7168]{3,2,0,1:T(8,128)(2,1)} %all-gather.5.cloned.1.call-done, bf16[5,256,3584]{2,1,0:T(8,128)(2,1)} %gather_fusion.13, bf16[5,256,3584]{2,1,0:T(8,128)(2,1)} %gather_fusion.12, f32[5,256,4,8]{1,3,2,0:T(8,128)S(1)} %fusion.9), kind=kOutput, calls=%fused_computation.48 | convolution fusion | flops 624148480 | bytes 20889600 | tf_op jit(solution)/shard_map/srcd,rfd->rfsc/dot_general | solution.py:109
  308.7 11.5 %all_gather.15 = bf16[5,2048,32]{1,2,0:T(8,128)(2,1)S(1)} all-gather(bf16[5,256,32]{1,2,0:T(8,128)(2,1)S(1)} %fusion.28), channel_id=1, replica_groups=mesh['ep'=8,'dp'=4] {'ep'}, dimensions={1}, use_global_device_ids=true | all-gather | bytes 737280 | tf_op jit(solution)/shard_map/all_gather | solution.py:121
  320.1 10.5 %fusion.21 = bf16[5,4,8,896]{3,2,1,0:T(8,128)(2,1)S(1)} fusion(bf16[5,2048,32]{1,2,0:T(8,128)(2,1)S(1)} %all_gather.15, bf16[5,896,1024]{2,1,0:T(8,128)(2,1)} %gather_fusion.15, bf16[5,896,1024]{2,1,0:T(8,128)(2,1)} %gather_fusion.14), kind=kOutput, calls=%fused_computation.43 | convolution fusion | flops 624046080 | bytes 19292160 | tf_op jit(solution)/shard_map/rfs,rdf->rsd/dot_general | solution.py:119
  334.9 10.0 %all-to-all-done.3 = bf16[5,4,8,896]{3,2,0,1:T(8,128)(2,1)S(1)} async-done(((bf16[5,4,8,896]{3,2,0,1:T(8,128)(2,1)}), bf16[5,4,8,896]{3,2,0,1:T(8,128)(2,1)S(1)}, u32[]{:S(2)}, u32[]{:S(2)}) %all-to-all-start.3) | async-done | bytes 286752 | tf_op jit(solution)/shard_map/all_to_all | solution.py:126
  (104 shorter events, 90.2 us)
Async XLA Ops:
  33.1 55.7 %all-to-all-start = ((bf16[4,5,8,896]{3,2,1,0:T(8,128)(2,1)}), bf16[4,5,8,896]{3,2,1,0:T(8,128)(2,1)S(1)}, u32[]{:S(2)}, u32[]{:S(2)}) async-start(bf16[4,5,8,896]{3,2,1,0:T(8,128)(2,1)} %bitcast.9), calls=%async_computation | async-start | bytes 573440 | tf_op jit(solution)/shard_map/all_to_all | solution.py:104
  37.9 116.0 %all-gather.3.cloned.1.call-start = ((), (), s32[]{:S(2)}) async-start(), calls=%async_computation.4 | async-start | bytes 2580480 | tf_op jit(solution)/shard_map/all_gather | solution.py:105
  62.2 7.7 %copy-start.2 = (s32[2,4,2]{1,2,0:T(2,128)S(1)}, s32[2,4,2]{1,2,0:T(2,128)}, u32[]{:S(2)}) copy-start(s32[2,4,2]{1,2,0:T(2,128)} %param.14) | copy-start | bytes 196
  145.8 7.7 %copy-start.1 = (s32[2,16,8]{1,2,0:T(8,128)S(1)}, s32[2,16,8]{1,2,0:T(8,128)}, u32[]{:S(2)}) copy-start(s32[2,16,8]{1,2,0:T(8,128)} %param.17) | copy-start | bytes 3076
  185.3 28.8 %copy-start = (bf16[16,896]{1,0:T(8,128)(2,1)S(1)}, bf16[16,896]{1,0:T(8,128)(2,1)}, u32[]{:S(2)}) copy-start(bf16[16,896]{1,0:T(8,128)(2,1)} %param.9) | copy-start | bytes 86020
  196.5 16.5 %all-to-all-start.1 = ((bf16[5,4,8,896]{3,2,0,1:T(8,128)(2,1)}), bf16[5,4,8,896]{3,2,0,1:T(8,128)(2,1)S(1)}, u32[]{:S(2)}, u32[]{:S(2)}) async-start(bf16[5,4,8,896]{3,2,0,1:T(8,128)(2,1)} %copy.53), calls=%async_computation.1 | async-start | bytes 573440 | tf_op jit(solution)/shard_map/all_to_all | solution.py:126
  203.0 85.0 %all-gather.5.cloned.1.call-start = ((), (), s32[]{:S(2)}) async-start(), calls=%async_computation.5 | async-start | bytes 2580480 | tf_op jit(solution)/shard_map/all_gather | solution.py:105
  331.3 13.6 %all-to-all-start.3 = ((bf16[5,4,8,896]{3,2,0,1:T(8,128)(2,1)}), bf16[5,4,8,896]{3,2,0,1:T(8,128)(2,1)S(1)}, u32[]{:S(2)}, u32[]{:S(2)}) async-start(bf16[5,4,8,896]{3,2,0,1:T(8,128)(2,1)} %copy.61), calls=%async_computation.3 | async-start | bytes 573440 | tf_op jit(solution)/shard_map/all_to_all | solution.py:126
Sparse Core Ops, SparseCore 0:
  89.7 28.5 all-gather.2
  239.3 26.7 all-gather.4
where the time goes:
time: 354 us
  local copies, waits for them, and re-layouts  172 us (49%)
  matrix products  64.4 us (18%)
  blocking collectives  60.9 us (17%)
  waiting for transfers between devices  19.8 us (6%)
  starting transfers between devices  14.9 us (4%)
  between operations  14.3 us (4%)
  other arithmetic  6.96 us (2%)
    gather x5, local copies, waits for them, and re-layouts, per_device(): up_all = up_weight[layer_id][chosen_ids]  48.1 us
    gather x5, local copies, waits for them, and re-layouts, per_device(): down_all = down_weight[layer_id][chosen_ids]  39.5 us
    gather x5, local copies, waits for them, and re-layouts, per_device(): gate_all = gate_weight[layer_id][chosen_ids]  39.4 us
    psum x2, blocking collectives, per_device(): squares = lax.psum(jnp.sum(stream_f * stream_f, axis=1), 'ep')  26.9 us
    all_gather x2, blocking collectives, per_device(): lax.all_gather(hidden, 'ep', axis=1, tiled=True)  21.9 us
    dot_general x2, matrix products, per_device(): jnp.einsum('rfs,rdf->rsd', lax.all_gather(hidden, 'ep', axis=1, tiled=Tru...  20.9 us
    dot_general x2, matrix products, per_device(): jnp.einsum('srcd,rfd->rfsc', portion, up_all, preferred_element_type=jnp....  20.8 us
    dot_general x2, matrix products, per_device(): jnp.einsum('srcd,rfd->rfsc', portion, gate_all, preferred_element_type=jn...  20.6 us
  transfers between devices with their start and end apart: 5, of which 2 were waited for; matrix products, arithmetic and copies ran while one was open for 46% of the time, Pallas kernels for 0%

commit v1 on v0

--- a/solution.py
+++ b/solution.py
@@ -1,7 +1,11 @@
 import jax
 import jax.numpy as jnp
 from jax import lax
+from jax.experimental import pallas as pl
+from jax.experimental.pallas import tpu as pltpu
 from jax.sharding import PartitionSpec as P
+
+import functools
 
 epsilon = 1e-06
 
@@ -135,9 +139,391 @@
     return (stream, update.astype(jnp.bfloat16))
 
 
+MESH_ID = pl.DeviceIdType.MESH
+NT = (((1,), (1,)), ((), ()))
+DIRECT = (1, 2, 4, 6)
+
+
+def kernel(
+    dims,
+    plan_ref,
+    tok_ref,
+    gain_ref,
+    route_ref,
+    pick_ref,
+    num_ref,
+    gate_hbm,
+    up_hbm,
+    down_hbm,
+    out_ref,
+    last_ref,
+    gate_buf,
+    up_buf,
+    down_buf,
+    xg,
+    xs,
+    hid,
+    cw,
+    part_f,
+    part_b,
+    got,
+    new_tok,
+    gate_sem,
+    up_sem,
+    down_sem,
+    z_send,
+    z_recv,
+    c_send,
+    c_recv,
+    p_send,
+    p_recv,
+    h_send,
+    h_recv,
+    r_send,
+    r_recv,
+):
+    n_dp, layers, experts, rep, top, capacity = dims
+    rows, width = tok_ref.shape
+    units = gate_hbm.shape[2]
+    features = gate_hbm.shape[3]
+    f32 = jnp.float32
+    me = lax.axis_index("ep")
+    host = lax.axis_index("dp")
+    bit_c = me % 2
+    bit_x = (me // 2) % 2
+    bit_y = me // 4
+
+    def peer(rel):
+        to = me
+        if rel & 1:
+            to = to + 1 - 2 * bit_c
+        if rel & 2:
+            to = to + 2 - 4 * bit_x
+        if rel & 4:
+            to = to + 4 - 8 * bit_y
+        return to
+
+    def fetch(hbm, buf, sem, layer, e, slot):
+        return pltpu.make_async_copy(hbm.at[layer, e], buf.at[slot, e], sem.at[layer, e])
+
+    for e in range(experts):
+        fetch(gate_hbm, gate_buf, gate_sem, 0, e, 0).start()
+        fetch(up_hbm, up_buf, up_sem, 0, e, 0).start()
+
+    barrier = pltpu.get_barrier_semaphore()
+    for k in range(1, n_dp):
+        pl.semaphore_signal(
+            barrier, inc=1, device_id={"dp": (host + k) % n_dp}, device_id_type=MESH_ID
+        )
+    for rel in range(1, 8):
+        pl.semaphore_signal(barrier, inc=1, device_id={"ep": peer(rel)}, device_id_type=MESH_ID)
+    pl.semaphore_wait(barrier, n_dp + 6)
+
+    def block(layer, slot, group):
+        lane = pl.multiple_of(slot * width, 128)
+        row = pl.multiple_of(group * rows, rows)
+        return xg.at[layer, pl.ds(row, rows), pl.ds(lane, width)]
+
+    def z_copy(layer, src, k, group):
+        return pltpu.make_async_remote_copy(
+            src_ref=src,
+            dst_ref=block(layer, me, group),
+            send_sem=z_send.at[layer, k],
+            recv_sem=z_recv.at[layer, k],
+            device_id={"dp": (host + k) % n_dp},
+            device_id_type=MESH_ID,
+        )
+
+    def p_copy(layer, k, slot, to, send, recv):
+        ref = block(layer, slot, (host + n_dp - k) % n_dp)
+        return pltpu.make_async_remote_copy(
+            src_ref=ref,
+            dst_ref=ref,
+            send_sem=p_send.at[layer, k, send],
+            recv_sem=p_recv.at[layer, k, recv],
+            device_id={"ep": peer(to)},
+            device_id_type=MESH_ID,
+        )
+
+    def c_copy(k, group):
+        row = pl.multiple_of(group * rows, rows)
+        ref = cw.at[:, pl.ds(row, rows), :]
+        return pltpu.make_async_remote_copy(
+            src_ref=ref,
+            dst_ref=ref,
+            send_sem=c_send.at[k],
+            recv_sem=c_recv.at[k],
+            device_id={"dp": (host + k) % n_dp},
+            device_id_type=MESH_ID,
+        )
+
+    def h_copy(layer, e, slot, rel):
+        lane = pl.multiple_of(slot * units, 128)
+        ref = hid.at[layer, e, :, pl.ds(lane, units)]
+        return pltpu.make_async_remote_copy(
+            src_ref=ref,
+            dst_ref=ref,
+            send_sem=h_send.at[layer, e, rel],
+            recv_sem=h_recv.at[layer, e, rel],
+            device_id={"ep": peer(rel)},
+            device_id_type=MESH_ID,
+        )
+
+    def r_copy(layer, k, group):
+        row = pl.multiple_of(group * rows, rows)
+        return pltpu.make_async_remote_copy(
+            src_ref=part_b.at[layer, pl.ds(row, rows), :],
+            dst_ref=got.at[layer, k],
+            send_sem=r_send.at[layer, k],
+            recv_sem=r_recv.at[layer, k],
+            device_id={"dp": (host + k) % n_dp},
+            device_id_type=MESH_ID,
+        )
+
+    def combine_weights(layer):
+        count = rows * top
+        reps = experts + rep
+        pad = 32
+        slot_t = lax.broadcasted_iota(jnp.int32, (pad, count), 0)
+        table = (slot_t // reps) * experts + slot_t % reps
+        for h in range(n_dp):
+            for q in range(rep):
+                base = ((h - 1 - q) % n_dp) * experts
+                served = base + plan_ref[(layer * n_dp + h) * rep + q]
+                table = jnp.where(slot_t == h * reps + experts + q, served, table)
+        table = jnp.where(slot_t < n_dp * reps, table, -1)
+        line = lax.broadcasted_iota(jnp.int32, route_ref.shape, 0) == layer * n_dp + host
+        expert_of = jnp.sum(jnp.where(line, route_ref[...], 0), axis=0, keepdims=True)
+        pick = jnp.sum(jnp.where(line, pick_ref[...], 0), axis=0, keepdims=True).astype(f32)
+        which = lax.broadcasted_iota(jnp.int32, num_ref.shape, 0) == layer
+        number = jnp.sum(jnp.where(which, num_ref[...], 0), axis=0, keepdims=True).astype(f32)
+        matches = jnp.where(table == expert_of, 1.0, 0.0)
+        counts = jnp.sum(matches, axis=0, keepdims=True)
+        t_a = lax.broadcasted_iota(jnp.int32, (pad, pad), 0)
+        t_b = lax.broadcasted_iota(jnp.int32, (pad, pad), 1)
+        below = jnp.where(t_b < t_a, 1.0, 0.0)
+        rank = jnp.dot(below, matches, preferred_element_type=f32)
+        wanted = pick - counts * jnp.floor((pick + 0.5) / counts)
+        chosen = matches * jnp.where(jnp.abs(rank - wanted) < 0.5, 1.0, 0.0)
+        s_a = lax.broadcasted_iota(jnp.int32, (count, count), 0)
+        s_b = lax.broadcasted_iota(jnp.int32, (count, count), 1)
+        earlier = jnp.where(s_a < s_b, 1.0, 0.0)
+        before = jnp.dot(chosen, earlier, preferred_element_type=f32)
+        position = jnp.sum(before * chosen, axis=0, keepdims=True)
+        same = jnp.where(s_a // top == s_b // top, 1.0, 0.0)
+        number8 = jnp.broadcast_to(number, (8, count))
+        total = jnp.dot(number8, same, preferred_element_type=f32)[0:1, :]
+        weight = jnp.where(position < capacity - 0.5, number / total, 0.0)
+        n_a = lax.broadcasted_iota(jnp.int32, (rows, count), 0)
+        n_b = lax.broadcasted_iota(jnp.int32, (rows, count), 1)
+        spread = jnp.where(n_b // top == n_a, weight, 0.0)
+        e_a = lax.broadcasted_iota(jnp.int32, (128, count), 0)
+        onehot = jnp.where(e_a == expert_of, 1.0, 0.0)
+        row = pl.multiple_of(host * rows, rows)
+        cw[layer, pl.ds(row, rows), :] = lax.dot_general(
+            spread, onehot, NT, preferred_element_type=f32, precision=lax.Precision.HIGHEST
+        )
+
+    lane_w = pl.multiple_of(me * width, 128)
+    row_h = pl.multiple_of(host * rows, rows)
+    for layer in range(layers):
+        src = tok_ref if layer == 0 else new_tok
+        for k in range(1, n_dp):
+            z_copy(layer, src, k, host).start()
+        xg[layer, pl.ds(row_h, rows), pl.ds(lane_w, width)] = src[...]
+        for i, rel in enumerate(DIRECT):
+            p_copy(layer, 0, me, rel, i, rel - 1).start()
+        if layer == 0:
+            for e in range(experts):
+                fetch(down_hbm, down_buf, down_sem, 0, e, 0).start()
+            for later in range(1, layers):
+                for e in range(experts):
+                    fetch(gate_hbm, gate_buf, gate_sem, later, e, later).start()
+                    fetch(up_hbm, up_buf, up_sem, later, e, later).start()
+            for each in range(layers):
+                combine_weights(each)
+            for k in range(1, n_dp):
+                c_copy(k, host).start()
+        for k in range(1, n_dp):
+            z_copy(layer, src, k, (host + n_dp - k) % n_dp).wait_recv()
+            for i, rel in enumerate(DIRECT):
+                p_copy(layer, k, me, rel, i, rel - 1).start()
+        for k in range(n_dp):
+            for i, rel in enumerate((2, 4, 6)):
+                p_copy(layer, k, peer(rel), rel, 0, rel - 1).wait_recv()
+                p_copy(layer, k, peer(rel), 1, 4 + i, rel).start()
+        for k in range(n_dp):
+            for rel in (1, 3, 5, 7):
+                p_copy(layer, k, peer(rel), rel, 0, rel - 1).wait_recv()
+        if layer == 0:
+            for k in range(1, n_dp):
+                c_copy(k, (host + n_dp - k) % n_dp).wait_recv()
+
+        squares = jnp.zeros((n_dp * rows, 1), f32)
+        for j in range(8):
+            lane = slice(j * width, (j + 1) * width)
+            x = xg[layer, :, lane].astype(f32)
+            gained = x.reshape(-1, 8, width) * gain_ref[layer, :, lane][None]
+            xs[:, lane] = gained.reshape(-1, width).astype(jnp.bfloat16)
+            squares = squares + jnp.sum(x * x, axis=1, keepdims=True)
+        inverse = lax.rsqrt(squares / features + epsilon)
+        weights = cw[layer]
+        column = lax.broadcasted_iota(jnp.int32, weights.shape, 1)
+
+        def expert(e, carry):
+            mine = jnp.where(column == host * experts + e, weights, 0.0)
+            mine = jnp.sum(mine, axis=1, keepdims=True)
+            fetch(gate_hbm, gate_buf, gate_sem, layer, e, layer).wait()
+            gate = lax.dot_general(xs[...], gate_buf[layer, e], NT, preferred_element_type=f32)
+            fetch(up_hbm, up_buf, up_sem, layer, e, layer).wait()
+            up = lax.dot_general(xs[...], up_buf[layer, e], NT, preferred_element_type=f32)
+            gate = gate * inverse
+            hidden = gate / (1.0 + jnp.exp(-gate)) * (up * inverse) * mine
+            lane = pl.multiple_of(me * units, 128)
+            hid[layer, e, :, pl.ds(lane, units)] = hidden.astype(jnp.bfloat16)
+            for rel in (6, 7, 2, 3, 4, 5, 1):
+                h_copy(layer, e, me, rel).start()
+            return carry
+
+        lax.fori_loop(0, experts, expert, 0)
+        part_f[...] = jnp.zeros_like(part_f)
+
+        def project(e, carry):
+            for rel in range(1, 8):
+                h_copy(layer, e, peer(rel), rel).wait_recv()
+            fetch(down_hbm, down_buf, down_sem, layer, e, 0).wait()
+            part_f[...] += lax.dot_general(
+                hid[layer, e], down_buf[0, e], NT, preferred_element_type=f32
+            )
+            if layer + 1 < layers:
+                fetch(down_hbm, down_buf, down_sem, layer + 1, e, 0).start()
+            return carry
+
+        lax.fori_loop(0, experts, project, 0)
+        part_b[layer] = part_f[...].astype(jnp.bfloat16)
+        for k in range(1, n_dp):
+            r_copy(layer, k, (host + k) % n_dp).start()
+        update = part_f[pl.ds(row_h, rows), :]
+        for k in range(1, n_dp):
+            r_copy(layer, k, host).wait_recv()
+        for k in range(1, n_dp):
+            update = update + got[layer, k].astype(f32)
+        stream = (src[...].astype(f32) + update).astype(jnp.bfloat16)
+        if layer + 1 < layers:
+            new_tok[...] = stream
+        else:
+            out_ref[...] = stream
+            last_ref[...] = update.astype(jnp.bfloat16)
+
+    for layer in range(layers):
+        src = tok_ref if layer == 0 else new_tok
+        for k in range(1, n_dp):
+            z_copy(layer, src, k, host).wait_send()
+            r_copy(layer, k, (host + k) % n_dp).wait_send()
+        for k in range(n_dp):
+            for i, rel in enumerate(DIRECT):
+                p_copy(layer, k, me, rel, i, rel - 1).wait_send()
+            for i, rel in enumerate((2, 4, 6)):
+                p_copy(layer, k, peer(rel), 1, 4 + i, rel).wait_send()
+        for e in range(experts):
+            for rel in range(1, 8):
+                h_copy(layer, e, me, rel).wait_send()
+    for k in range(1, n_dp):
+        c_copy(k, host).wait_send()
+
+
+def fused(
+    tokens,
+    norm_gain,
+    gate_weight,
+    up_weight,
+    down_weight,
+    replica_plan,
+    route_expert,
+    replica_pick,
+    combine_num,
+):
+    n_dp = lax.axis_size("dp")
+    layers, features = norm_gain.shape
+    rows, width = tokens.shape
+    experts, units = gate_weight.shape[1:3]
+    inner = down_weight.shape[3]
+    rep = replica_plan.shape[2]
+    top = route_expert.shape[2]
+    count = n_dp * rows
+    dims = (n_dp, layers, experts, rep, top, rows // 2)
+    bf16 = jnp.bfloat16
+    vmem = pl.BlockSpec(memory_space=pltpu.VMEM)
+    dma = pltpu.SemaphoreType.DMA
+    return pl.pallas_call(
+        functools.partial(kernel, dims),
+        out_shape=(
+            jax.ShapeDtypeStruct((rows, width), bf16),
+            jax.ShapeDtypeStruct((rows, width), bf16),
+        ),
+        in_specs=[pl.BlockSpec(memory_space=pltpu.SMEM)]
+        + [vmem] * 5
+        + [pl.BlockSpec(memory_space=pl.ANY)] * 3,
+        out_specs=(vmem, vmem),
+        scratch_shapes=[
+            pltpu.VMEM((layers, experts, units, features), bf16),
+            pltpu.VMEM((layers, experts, units, features), bf16),
+            pltpu.VMEM((1, experts, width, inner), bf16),
+            pltpu.VMEM((layers, count, features), bf16),
+            pltpu.VMEM((count, features), bf16),
+            pltpu.VMEM((layers, experts, count, inner), bf16),
+            pltpu.VMEM((layers, count, 128), jnp.float32),
+            pltpu.VMEM((count, width), jnp.float32),
+            pltpu.VMEM((layers, count, width), bf16),
+            pltpu.VMEM((layers, n_dp, rows, width), bf16),
+            pltpu.VMEM((rows, width), bf16),
+            dma((layers, experts)),
+            dma((layers, experts)),
+            dma((layers, experts)),
+            dma((layers, n_dp)),
+            dma((layers, n_dp)),
+            dma((n_dp,)),
+            dma((n_dp,)),
+            dma((layers, n_dp, 7)),
+            dma((layers, n_dp, 7)),
+            dma((layers, experts, 8)),
+            dma((layers, experts, 8)),
+            dma((layers, n_dp)),
+            dma((layers, n_dp)),
+        ],
+        compiler_params=pltpu.CompilerParams(
+            collective_id=0, has_side_effects=True, vmem_limit_bytes=67043328
+        ),
+        name="moe_layers",
+    )(
+        replica_plan.reshape(-1),
+        tokens,
+        jnp.broadcast_to(norm_gain[:, None, :], (layers, 8, features)),
+        route_expert.reshape(layers * n_dp, rows * top),
+        replica_pick.reshape(layers * n_dp, rows * top),
+        jnp.pad(combine_num.reshape(layers, rows * top), ((0, -layers % 8), (0, 0))),
+        gate_weight,
+        up_weight,
+        down_weight,
+    )
+
+
+def device_step(*arrays):
+    tokens, gate_weight, route_expert = arrays[0], arrays[2], arrays[6]
+    rows, width = tokens.shape
+    fits = (
+        lax.axis_size("ep") == 8
+        and width % 128 == 0
+        and gate_weight.shape[2] % 128 == 0
+        and rows % 16 == 0
+        and rows * route_expert.shape[2] == 128
+    )
+    return fused(*arrays) if fits else per_device(*arrays)
+
+
 def solution(mesh):
     return jax.shard_map(
-        per_device,
+        device_step,
         mesh=mesh,
         in_specs=(
             P("dp", "ep"),

time: 354 us -> 85.7 us (0.24)
  local copies, waits for them, and re-layouts: 172 us -> 10.2 us
  Pallas kernels: 0 us -> 74.4 us
  matrix products: 64.4 us -> 0 us
  blocking collectives: 60.9 us -> 0 us
  waiting for transfers between devices: 19.8 us -> 0 us
  starting transfers between devices: 14.9 us -> 0 us
  between operations: 14.3 us -> 0.66 us
  other arithmetic: 6.96 us -> 0 us
    gather x19 -> x0, local copies, waits for them, and re-layouts: 130 us -> none  [the longest x5 48.1 us: per_device(): up_all = up_weight[layer_id][chosen_ids]]
    pallas_call x0 -> x1, Pallas kernels: none -> 74.4 us  [fused(): pl.pallas_call(functools.partial(kernel, dims), out_shape=(jax.ShapeDtype...]
    dot_general x8 -> x0, matrix products: 64.4 us -> none  [the longest x2 20.9 us: per_device(): jnp.einsum('rfs,rdf->rsd', lax.all_gather(hidden, 'ep', axis=1, tiled=Tru...]
    squeeze x4 -> x0, local copies, waits for them, and re-layouts: 34 us -> none  [the longest x1 15.5 us: per_device(): up_all = up_weight[layer_id][chosen_ids]]
    psum x2 -> x0, blocking collectives: 26.9 us -> none  [per_device(): squares = lax.psum(jnp.sum(stream_f * stream_f, axis=1), 'ep')]
    all_gather x2 -> x0, blocking collectives: 21.9 us -> none  [per_device(): lax.all_gather(hidden, 'ep', axis=1, tiled=True)]
    all_to_all x3 -> x0, waiting for transfers between devices: 19.8 us -> none  [the longest x2 19.7 us: per_device(): lax.all_to_all(result, 'dp', split_axis=1, concat_axis=1, tiled=True)]
    all_to_all x3 -> x0, starting transfers between devices: 14.9 us -> none  [the longest x2 10 us: per_device(): lax.all_to_all(result, 'dp', split_axis=1, concat_axis=1, tiled=True)]
  transfers between devices with their start and end apart: 5 -> 0, of which waited for: 2 -> 0; matrix products, arithmetic and copies ran while one was open for 46% -> 0% of each run, Pallas kernels for 0% -> 0%
where the time goes in v1:
time: 85.7 us; the launch traced here: 85.2 us
  Pallas kernels  74.4 us (87%)
  local copies, waits for them, and re-layouts  10.2 us (12%)
    pallas_call x1, Pallas kernels, fused(): pl.pallas_call(functools.partial(kernel, dims), out_shape=(jax.ShapeDtype...  74.4 us
    unnamed x6, local copies, waits for them, and re-layouts  5.83 us

profile of v1, /device:TPU:0, one launch (start us, length us, event | category | flops | bytes accessed | tf_op | source)
XLA Modules:
  0.0 85.2 jit_solution(17423332127069527552)
XLA Ops:
  0.6 0.8 copy.15
  1.4 0.7 reshape.17.plan_ref
  2.1 0.8 copy.18
  2.8 0.1 reshape.20
  2.9 0.6 pad.4.num_ref
  3.5 0.8 copy.16
  4.3 0.7 reshape.18.route_ref
  5.0 0.8 copy.17
  5.8 0.7 reshape.19.pick_ref
  6.5 1.6 %broadcast_in_dim.2.gain_ref = f32[2,8,7168]{2,1,0:T(8,128)} broadcast(f32[2,7168]{1,0:T(2,128)} %param.10), dimensions={0,2} | broadcast | bytes 516096 | tf_op jit(solution)/shard_map/broadcast_in_dim | solution.py:501
  8.1 74.4 %moe_layers.1 = (bf16[16,896]{1,0:T(8,128)(2,1)}, bf16[16,896]{1,0:T(8,128)(2,1)}) custom-call(s32[16]{0:T(128)} %reshape.17.plan_ref, bf16[16,896]{1,0:T(8,128)(2,1)} %tok_ref.1, f32[2,8,7168]{2,1,0:T(8,128)} %broadcast_in_dim.2.gain_ref, s32[8,128]{1,0:T(8,128)} %reshape.18.route_ref, s32[8,128]{1,0:T(8,128)} %reshape.19.pick_ref, s32[8,128]{1,0:T(8,128)} %pad.4.num_ref, ...), custom_call_target="tpu_custom_call" | custom-call | tf_op jit(solution)/shard_map/moe_layers/pallas_call | solution.py:458
  82.5 1.4 %copy.21 = bf16[16,896]{1,0:T(8,128)(2,1)} copy(bf16[16,896]{1,0:T(8,128)(2,1)} %get-tuple-element.4) | data formatting | bytes 57344
  83.9 1.4 %copy.22 = bf16[16,896]{1,0:T(8,128)(2,1)} copy(bf16[16,896]{1,0:T(8,128)(2,1)} %get-tuple-element.5) | data formatting | bytes 57344

commit v2 on v1

--- a/solution.py
+++ b/solution.py
@@ -149,9 +149,7 @@
     plan_ref,
     tok_ref,
     gain_ref,
-    route_ref,
-    pick_ref,
-    num_ref,
+    ints_ref,
     gate_hbm,
     up_hbm,
     down_hbm,
@@ -292,11 +290,15 @@
                 served = base + plan_ref[(layer * n_dp + h) * rep + q]
                 table = jnp.where(slot_t == h * reps + experts + q, served, table)
         table = jnp.where(slot_t < n_dp * reps, table, -1)
-        line = lax.broadcasted_iota(jnp.int32, route_ref.shape, 0) == layer * n_dp + host
-        expert_of = jnp.sum(jnp.where(line, route_ref[...], 0), axis=0, keepdims=True)
-        pick = jnp.sum(jnp.where(line, pick_ref[...], 0), axis=0, keepdims=True).astype(f32)
-        which = lax.broadcasted_iota(jnp.int32, num_ref.shape, 0) == layer
-        number = jnp.sum(jnp.where(which, num_ref[...], 0), axis=0, keepdims=True).astype(f32)
+        lines = layers * n_dp
+        row_of = lax.broadcasted_iota(jnp.int32, (lines, count), 0)
+        line = row_of == layer * n_dp + host
+        routes, picks = ints_ref[0:lines, :], ints_ref[lines : 2 * lines, :]
+        numbers = ints_ref[2 * lines : 3 * lines, :]
+        expert_of = jnp.sum(jnp.where(line, routes, 0), axis=0, keepdims=True)
+        pick = jnp.sum(jnp.where(line, picks, 0), axis=0, keepdims=True).astype(f32)
+        number = jnp.sum(jnp.where(row_of == layer, numbers, 0), axis=0, keepdims=True)
+        number = number.astype(f32)
         matches = jnp.where(table == expert_of, 1.0, 0.0)
         counts = jnp.sum(matches, axis=0, keepdims=True)
         t_a = lax.broadcasted_iota(jnp.int32, (pad, pad), 0)
@@ -340,10 +342,6 @@
                 for e in range(experts):
                     fetch(gate_hbm, gate_buf, gate_sem, later, e, later).start()
                     fetch(up_hbm, up_buf, up_sem, later, e, later).start()
-            for each in range(layers):
-                combine_weights(each)
-            for k in range(1, n_dp):
-                c_copy(k, host).start()
         for k in range(1, n_dp):
             z_copy(layer, src, k, (host + n_dp - k) % n_dp).wait_recv()
             for i, rel in enumerate(DIRECT):
@@ -352,6 +350,11 @@
             for i, rel in enumerate((2, 4, 6)):
                 p_copy(layer, k, peer(rel), rel, 0, rel - 1).wait_recv()
                 p_copy(layer, k, peer(rel), 1, 4 + i, rel).start()
+        if layer == 0:
+            for each in range(layers):
+                combine_weights(each)
+            for k in range(1, n_dp):
+                c_copy(k, host).start()
         for k in range(n_dp):
             for rel in (1, 3, 5, 7):
                 p_copy(layer, k, peer(rel), rel, 0, rel - 1).wait_recv()
@@ -453,6 +456,15 @@
     count = n_dp * rows
     dims = (n_dp, layers, experts, rep, top, rows // 2)
     bf16 = jnp.bfloat16
+    lines = layers * n_dp
+    own = combine_num.reshape(layers, rows * top)
+    ints = jnp.concatenate(
+        [
+            route_expert.reshape(lines, rows * top),
+            replica_pick.reshape(lines, rows * top),
+            jnp.pad(own, ((0, lines - layers), (0, 0))),
+        ]
+    )
     vmem = pl.BlockSpec(memory_space=pltpu.VMEM)
     dma = pltpu.SemaphoreType.DMA
     return pl.pallas_call(
@@ -462,7 +474,7 @@
             jax.ShapeDtypeStruct((rows, width), bf16),
         ),
         in_specs=[pl.BlockSpec(memory_space=pltpu.SMEM)]
-        + [vmem] * 5
+        + [vmem] * 3
         + [pl.BlockSpec(memory_space=pl.ANY)] * 3,
         out_specs=(vmem, vmem),
         scratch_shapes=[
@@ -499,9 +511,7 @@
         replica_plan.reshape(-1),
         tokens,
         jnp.broadcast_to(norm_gain[:, None, :], (layers, 8, features)),
-        route_expert.reshape(layers * n_dp, rows * top),
-        replica_pick.reshape(layers * n_dp, rows * top),
-        jnp.pad(combine_num.reshape(layers, rows * top), ((0, -layers % 8), (0, 0))),
+        ints,
         gate_weight,
         up_weight,
         down_weight,
@@ -516,6 +526,7 @@
         and width % 128 == 0
         and gate_weight.shape[2] % 128 == 0
         and rows % 16 == 0
+        and arrays[1].shape[0] * lax.axis_size("dp") % 8 == 0
         and rows * route_expert.shape[2] == 128
     )
     return fused(*arrays) if fits else per_device(*arrays)

time: 85.7 us -> 87.1 us (1.016)
  Pallas kernels: 74.4 us -> 77 us
  local copies, waits for them, and re-layouts: 10.2 us -> 8.32 us
    pallas_call x1, Pallas kernels: 74.4 us -> 77 us  [fused(): pl.pallas_call(functools.partial(kernel, dims), out_shape=(jax.ShapeDtype...]
    reshape x3, local copies, waits for them, and re-layouts: 1.47 us -> 0.27 us  [the longest x1 0.09 us: fused(): route_expert.reshape(lines, rows * top)]
where the time goes in v2:
time: 87.1 us; the launch traced here: 86.6 us
  Pallas kernels  77 us (88%)
  local copies, waits for them, and re-layouts  8.32 us (10%)
    pallas_call x1, Pallas kernels, fused(): pl.pallas_call(functools.partial(kernel, dims), out_shape=(jax.ShapeDtype...  77 us
    unnamed x6, local copies, waits for them, and re-layouts  5.83 us

profile of v2, /device:TPU:0, one launch (start us, length us, event | category | flops | bytes accessed | tf_op | source)
XLA Modules:
  0.0 86.6 jit_solution(8739078372643109781)
XLA Ops:
  0.6 0.8 copy.15
  1.4 0.6 reshape.17.plan_ref
  2.0 0.8 copy.18
  2.8 0.1 reshape.20
  2.9 0.8 copy.16
  3.7 0.1 reshape.18
  3.8 0.8 copy.17
  4.6 0.1 reshape.19
  4.6 0.6 pad_add_fusion.ints_ref
  5.3 1.6 %broadcast_in_dim.2.gain_ref = f32[2,8,7168]{2,1,0:T(8,128)} broadcast(f32[2,7168]{1,0:T(2,128)} %param.10), dimensions={0,2} | broadcast | bytes 516096 | tf_op jit(solution)/shard_map/broadcast_in_dim | solution.py:513
  6.9 77.0 %moe_layers.1 = (bf16[16,896]{1,0:T(8,128)(2,1)}, bf16[16,896]{1,0:T(8,128)(2,1)}) custom-call(s32[16]{0:T(128)} %reshape.17.plan_ref, bf16[16,896]{1,0:T(8,128)(2,1)} %tok_ref.1, f32[2,8,7168]{2,1,0:T(8,128)} %broadcast_in_dim.2.gain_ref, s32[24,128]{1,0:T(8,128)} %pad_add_fusion.ints_ref, bf16[2,3,256,7168]{3,2,1,0:T(8,128)(2,1)} %gate_hbm.1, ...), custom_call_target="tpu_custom_call" | custom-call | tf_op jit(solution)/shard_map/moe_layers/pallas_call | solution.py:470
  83.9 1.4 %copy.21 = bf16[16,896]{1,0:T(8,128)(2,1)} copy(bf16[16,896]{1,0:T(8,128)(2,1)} %get-tuple-element.4) | data formatting | bytes 57344
  85.2 1.4 %copy.22 = bf16[16,896]{1,0:T(8,128)(2,1)} copy(bf16[16,896]{1,0:T(8,128)(2,1)} %get-tuple-element.5) | data formatting | bytes 57344
